TPU v7x, 32 devices: a whole 2x2x4 slice. The times are simulated.
32 devices in a mesh: row: 8 (over z, y), col: 4 (over x, core).
Axes of the slice: x: 2, y: 2, z: 4, core: 2. Of those that a mesh axis runs over, the one named last changes fastest.
Arguments:
- tile_values: bfloat16 [128, 8, 256, 256], P(('row', 'col')), may hold values from -0.375 to 0.375
- block_columns: int32 [128, 8], P(('row', 'col')), may hold values from 0 to 127, as said below
- tile_counts: int32 [128], P(('row', 'col')), may hold values from 1 to 8, as said below
- diagonal: float32 [32768], P(('row', 'col')), may hold values from 0.5 to 4
- sketch_rows: int32 [32768], P(('row', 'col')), may hold values from 0 to 1023
- sketch_signs: int32 [32768], P(('row', 'col')), may hold values from 0 to 1
- right_side: float32 [16, 32768], P(None, ('row', 'col')), may hold values from -70 to 70
Outputs:
- solution: float32 [16, 32768], P(None, ('row', 'col'))
- last_basis: float32 [16, 32768], P(None, ('row', 'col'))
- hessenberg: float32 [16, 5, 4], replicated
Inputs may be any that keep to these rules, and one draw needn't show every extreme that they name: `block_columns`: for block row b all 8 entries are distinct block columns c with (c - b) mod 128 <= 4 or >= 124; only slots k < tile_counts[b] are used. `tile_counts`: in every draw the 4 block rows of at least one device all have 8.
All inputs are finite; a program needn't handle non-finite values.
Results may differ from a plain program's by a relative error of at most 0.0053.
Values may be sent and summed in bfloat16 or wider, within the bound.
A program may use at most 64 MiB of HBM per device.

v0:
```python
import functools
import math

import jax
import jax.numpy as jnp
from jax import lax
from jax.experimental import pallas as pl
from jax.experimental.pallas import tpu as pltpu
from jax.sharding import PartitionSpec as P

SKETCH = 1024
ITERS = 4
PARTS = 3
SHIFT = 1.75
epsilon = 1e-06
MESH = pl.DeviceIdType.MESH
f32 = jnp.float32
bf16 = jnp.bfloat16


def split_parts(value):
    parts = []
    for _ in range(PARTS - 1):
        head = value.astype(bf16)
        parts.append(head)
        value = value - head.astype(f32)
    parts.append(value.astype(bf16))
    return parts


def extend_factor(factor, inverse, entries):
    row = len(inverse)
    for column in range(row):
        entry = entries[column]
        for inner in range(column):
            entry = entry - factor[row, inner] * factor[column, inner]
        factor[row, column] = entry * inverse[column]
    diag_part = entries[row]
    for inner in range(row):
        diag_part = diag_part - factor[row, inner] * factor[row, inner]
    inverse.append(1.0 / jnp.sqrt(diag_part))


def factor_solve(factor, inverse, target):
    order = len(target)
    forward = []
    for column in range(order):
        entry = target[column]
        for inner in range(column):
            entry = entry - factor[column, inner] * forward[inner]
        forward.append(entry * inverse[column])
    result = [None] * order
    for column in reversed(range(order)):
        entry = forward[column]
        for inner in range(column + 1, order):
            entry = entry - factor[inner, column] * result[inner]
        result[column] = entry * inverse[column]
    return result


def inner_product(a, b):
    return jnp.sum(jnp.sum(a * b, axis=0), axis=1, keepdims=True)


def nt_dot(a, b):
    return lax.dot_general(a, b, (((1,), (1,)), ((), ())), preferred_element_type=f32)


def kernel(
    rows,
    cols,
    scaling,
    columns_hbm,
    counts_hbm,
    diag_hbm,
    rows_hbm,
    signs_hbm,
    right_hbm,
    tiles_hbm,
    solution_ref,
    last_ref,
    hess_ref,
    columns_ref,
    counts_ref,
    diag_ref,
    rows_ref,
    signs_ref,
    tiles,
    projector,
    krylov,
    window,
    index_ref,
    halo,
    part,
    land1,
    land2,
    sketches,
    load_sem,
    halo_send,
    halo_recv,
    send1,
    recv1,
    send2,
    recv2,
    send3,
    recv3,
):
    row = lax.axis_index("row")
    col = lax.axis_index("col")
    devices = rows * cols
    me = row * cols + col
    block_rows, slots, tile, _ = tiles.shape
    systems, width = right_hbm.shape
    all_blocks = block_rows * devices
    share = SKETCH // cols
    right = lax.rem(me + 1, devices)
    left = lax.rem(me + devices - 1, devices)
    right = (lax.div(right, cols), lax.rem(right, cols))
    left = (lax.div(left, cols), lax.rem(left, cols))
    col_to = [lax.rem(col + off, cols) for off in range(cols)]
    col_from = [lax.rem(col + cols - off, cols) for off in range(cols)]
    row_to = [lax.rem(row + off, rows) for off in range(rows)]
    row_from = [lax.rem(row + rows - off, rows) for off in range(rows)]

    barrier = pltpu.get_barrier_semaphore()
    for peer in (left, right):
        pl.semaphore_signal(barrier, inc=1, device_id=peer, device_id_type=MESH)
    for off in range(1, rows):
        pl.semaphore_signal(barrier, inc=1, device_id=(row_to[off], col), device_id_type=MESH)
    for off in range(1, cols):
        pl.semaphore_signal(barrier, inc=1, device_id=(row, col_to[off]), device_id_type=MESH)

    loads = [
        pltpu.make_async_copy(source, target, load_sem.at[n])
        for n, (source, target) in enumerate(
            [
                (rows_hbm, rows_ref),
                (signs_hbm, signs_ref),
                (columns_hbm, columns_ref),
                (counts_hbm, counts_ref),
                (diag_hbm, diag_ref),
            ]
            + [
                (right_hbm.at[:, pl.ds(b * tile, tile)], krylov.at[0, b])
                for b in range(block_rows)
            ]
            + [(tiles_hbm, tiles)]
        )
    ]
    for load in loads:
        load.start()
    for load in loads[:4]:
        load.wait()

    first = me * block_rows
    for b in range(block_rows):
        for slot in range(slots):
            spot = lax.rem(columns_ref[b, slot] - first + block_rows + all_blocks, all_blocks)
            index_ref[b * slots + slot] = jnp.where(slot < counts_ref[b], spot, 3 * block_rows)
    window[3 * block_rows] = jnp.zeros(window.shape[1:], window.dtype)

    signed = (2 * signs_ref[...] - 1).astype(f32)
    targets = rows_ref[...]
    chunk = 64

    def build(step, carry):
        base = pl.multiple_of(step * chunk, chunk)
        spots = lax.broadcasted_iota(jnp.int32, (chunk, width), 0) + base
        projector[pl.ds(base, chunk), :] = jnp.where(spots == targets, signed, 0.0).astype(bf16)
        return carry

    lax.fori_loop(0, SKETCH // chunk, build, 0)
    for load in loads[4:-1]:
        load.wait()
    pl.semaphore_wait(barrier, rows + cols)

    def halo_copies(k, b):
        return [
            pltpu.make_async_remote_copy(
                src_ref=krylov.at[k, b],
                dst_ref=halo.at[k, side, b],
                send_sem=halo_send.at[k, side, b],
                recv_sem=halo_recv.at[k, side, b],
                device_id=peer,
                device_id_type=MESH,
            )
            for side, peer in ((0, right), (1, left))
        ]

    def copy1(k, off, block):
        return pltpu.make_async_remote_copy(
            src_ref=part.at[k, block],
            dst_ref=land1.at[k, off - 1],
            send_sem=send1.at[k, off - 1],
            recv_sem=recv1.at[k, off - 1],
            device_id=(row, col_to[off]),
            device_id_type=MESH,
        )

    def copy2(k, off, source):
        return pltpu.make_async_remote_copy(
            src_ref=land2.at[k, source],
            dst_ref=land2.at[k, source],
            send_sem=send2.at[k, off - 1],
            recv_sem=recv2.at[k, off - 1],
            device_id=(row_to[off], col),
            device_id_type=MESH,
        )

    def copy3(k, off, source):
        return pltpu.make_async_remote_copy(
            src_ref=sketches.at[k, source],
            dst_ref=sketches.at[k, source],
            send_sem=send3.at[k, off - 1],
            recv_sem=recv3.at[k, off - 1],
            device_id=(row, col_to[off]),
            device_id_type=MESH,
        )

    def place(value, spot):
        window[spot] = jnp.concatenate(split_parts(value), axis=0)

    def stage1(k):
        for block in range(cols):
            total = None
            for b in range(block_rows):
                term = nt_dot(
                    window[block_rows + b],
                    projector[pl.ds(block * share, share), pl.ds(b * tile, tile)],
                )
                total = term if total is None else total + term
            summed = total[(PARTS - 1) * systems :]
            for p in reversed(range(PARTS - 1)):
                summed = summed + total[p * systems : (p + 1) * systems]
            part[k, block] = summed * scaling
        for off in range(1, cols):
            copy1(k, off, col_to[off]).start()

    def stage2(k):
        for off in range(1, cols):
            copy1(k, off, 0).wait_recv()
        total = part[k, col]
        for off in range(1, cols):
            total = total + land1[k, off - 1]
        land2[k, row] = total
        for off in range(1, rows):
            copy2(k, off, row).start()

    def stage3(k):
        for off in range(1, rows):
            copy2(k, off, row_from[off]).wait_recv()
        total = land2[k, 0]
        for r in range(1, rows):
            total = total + land2[k, r]
        sketches[k, col] = total
        for off in range(1, cols):
            copy3(k, off, col).start()

    def finish(k):
        for off in range(1, cols):
            copy3(k, off, col_from[off]).wait_recv()

    coords = []
    sketched = []
    factor, inverse = {}, []
    hess = {}
    normal, normal_inverse = {}, []

    def spread_of(j):
        spread = [SHIFT * entry for entry in coords[j - 1]] + [None]
        for i in range(j):
            moved = coords[j - 1][i]
            spread[i + 1] = moved if spread[i + 1] is None else spread[i + 1] + moved
        image = spread[0] * sketches[0]
        for i in range(1, j):
            image = image + spread[i] * sketches[i]
        return spread, image

    def arnoldi(j, prepared):
        spread, image = prepared
        image = image + spread[j] * sketches[j]
        coeffs = factor_solve(factor, inverse, [inner_product(q, image) for q in sketched])
        for i in range(j):
            image = image - coeffs[i] * sketched[i]
            for m in range(i + 1):
                spread[m] = spread[m] - coeffs[i] * coords[i][m]
        norm = jnp.sqrt(inner_product(image, image) + epsilon)
        scale = 1.0 / norm
        for i in range(j):
            hess[i, j - 1] = coeffs[i]
        hess[j, j - 1] = norm
        coords.append([entry * scale for entry in spread])
        if j < ITERS:
            add_sketched(image * scale)
        entries = []
        for n in range(j):
            entry = None
            for i in range(n + 2):
                term = hess[i, j - 1] * hess[i, n]
                entry = term if entry is None else entry + term
            entries.append(entry)
        extend_factor(normal, normal_inverse, entries)

    def add_sketched(q):
        sketched.append(q)
        extend_factor(factor, inverse, [inner_product(q, other) for other in sketched])

    for b in range(block_rows):
        for copy in halo_copies(0, b):
            copy.start()
    for b in range(block_rows):
        place(krylov[0, b], block_rows + b)
    beta = None
    for k in range(ITERS):
        stage1(k)
        if k >= 1:
            stage3(k - 1)
        if k == 2:
            finish(0)
            start = sketches[0]
            beta = jnp.sqrt(inner_product(start, start) + epsilon)
            coords.append([1.0 / beta])
            add_sketched(start * coords[0][0])
        if k >= 3:
            finish(k - 2)
            arnoldi(k - 2, spread_of(k - 2))
        stage2(k)
        for b in range(block_rows):
            for copy in halo_copies(k, b):
                copy.wait_recv()
            place(halo[k, 0, b], b)
            place(halo[k, 1, b], 2 * block_rows + b)
        if k == 0:
            loads[-1].wait()
        for b in range(block_rows):
            total = None
            for slot in range(slots):
                term = nt_dot(window[index_ref[b * slots + slot]], tiles[b, slot])
                total = term if total is None else total + term
            summed = total[(PARTS - 1) * systems :]
            for p in reversed(range(PARTS - 1)):
                summed = summed + total[p * systems : (p + 1) * systems]
            diag_b = diag_ref[0:1, pl.ds(b * tile, tile)] - SHIFT
            krylov[k + 1, b] = diag_b * krylov[k, b] + summed
            if k + 1 < ITERS:
                for copy in halo_copies(k + 1, b):
                    copy.start()
        for b in range(block_rows):
            place(krylov[k + 1, b], block_rows + b)
    stage1(ITERS)
    stage3(ITERS - 1)
    finish(ITERS - 2)
    arnoldi(ITERS - 2, spread_of(ITERS - 2))
    stage2(ITERS)
    finish(ITERS - 1)
    arnoldi(ITERS - 1, spread_of(ITERS - 1))
    prepared = spread_of(ITERS)
    stage3(ITERS)
    finish(ITERS)
    arnoldi(ITERS, prepared)

    lane = lax.broadcasted_iota(jnp.int32, (systems, 128), 1)
    packed = jnp.zeros((systems, 128), f32)
    for (i, j), value in hess.items():
        packed = jnp.where(lane == i * ITERS + j, value, packed)
    turned = packed.T
    for i in range(ITERS + 1):
        hess_ref[i] = turned[i * ITERS : (i + 1) * ITERS, :]

    weights = factor_solve(normal, normal_inverse, [beta * hess[0, n] for n in range(ITERS)])
    mixed = []
    for m in range(ITERS):
        entry = None
        for i in range(m, ITERS):
            term = weights[i] * coords[i][m]
            entry = term if entry is None else entry + term
        mixed.append(entry)
    for b in range(block_rows):
        lanes = pl.ds(b * tile, tile)
        out = mixed[0] * krylov[0, b]
        for m in range(1, ITERS):
            out = out + mixed[m] * krylov[m, b]
        solution_ref[:, lanes] = out
        out = coords[ITERS][0] * krylov[0, b]
        for m in range(1, ITERS + 1):
            out = out + coords[ITERS][m] * krylov[m, b]
        last_ref[:, lanes] = out

    for k in range(ITERS + 1):
        if k < ITERS:
            for b in range(block_rows):
                for copy in halo_copies(k, b):
                    copy.wait_send()
        for off in range(1, cols):
            copy1(k, off, col_to[off]).wait_send()
            copy3(k, off, col).wait_send()
        for off in range(1, rows):
            copy2(k, off, row).wait_send()


def local(
    rows, cols, tile_values, block_columns, tile_counts, diagonal, sketch_rows, sketch_signs, right_side
):
    block_rows, _, tile, _ = tile_values.shape
    systems, width = right_side.shape
    scaling = 1.0 / math.sqrt(width * rows * cols)
    share = SKETCH // cols
    vectors = ITERS + 1
    vmem = pl.BlockSpec(memory_space=pltpu.VMEM)
    hbm = pl.BlockSpec(memory_space=pltpu.HBM)
    dma = pltpu.SemaphoreType.DMA
    iterate, last, hessenberg = pl.pallas_call(
        functools.partial(kernel, rows, cols, scaling),
        out_shape=(
            pltpu.VMEM((systems, width), f32),
            pltpu.VMEM((systems, width), f32),
            pltpu.VMEM((ITERS + 1, ITERS, systems), f32),
        ),
        in_specs=[hbm] * 7,
        out_specs=(vmem, vmem, vmem),
        scratch_shapes=[
            pltpu.SMEM(block_columns.shape, jnp.int32),
            pltpu.SMEM(tile_counts.shape, jnp.int32),
            pltpu.VMEM((1, width), f32),
            pltpu.VMEM((1, width), jnp.int32),
            pltpu.VMEM((1, width), jnp.int32),
            pltpu.VMEM(tile_values.shape, bf16),
            pltpu.VMEM((SKETCH, width), bf16),
            pltpu.VMEM((vectors, block_rows, systems, tile), f32),
            pltpu.VMEM((3 * block_rows + 1, PARTS * systems, tile), bf16),
            pltpu.SMEM((tile_values.shape[0] * tile_values.shape[1],), jnp.int32),
            pltpu.VMEM((ITERS, 2, block_rows, systems, tile), f32),
            pltpu.VMEM((vectors, cols, systems, share), f32),
            pltpu.VMEM((vectors, cols - 1, systems, share), f32),
            pltpu.VMEM((vectors, rows, systems, share), f32),
            pltpu.VMEM((vectors, cols, systems, share), f32),
            dma((block_rows + 6,)),
            dma((ITERS, 2, block_rows)),
            dma((ITERS, 2, block_rows)),
            dma((vectors, cols - 1)),
            dma((vectors, cols - 1)),
            dma((vectors, rows - 1)),
            dma((vectors, rows - 1)),
            dma((vectors, cols - 1)),
            dma((vectors, cols - 1)),
        ],
        compiler_params=pltpu.CompilerParams(
            collective_id=0, has_side_effects=True, vmem_limit_bytes=67043328 - 160 * 1024
        ),
    )(
        block_columns,
        tile_counts,
        diagonal.reshape(1, width),
        sketch_rows.reshape(1, width),
        sketch_signs.reshape(1, width),
        right_side,
        tile_values,
    )
    return iterate, last, jnp.transpose(hessenberg, (2, 0, 1))


def solution(mesh):
    spec = P(("row", "col"))
    in_specs = (
        P(("row", "col"), None, None, None),
        P(("row", "col"), None),
        spec,
        spec,
        spec,
        spec,
        P(None, ("row", "col")),
    )
    out_specs = (P(None, ("row", "col")), P(None, ("row", "col")), P())
    body = functools.partial(local, mesh.shape["row"], mesh.shape["col"])
    return jax.shard_map(body, mesh=mesh, in_specs=in_specs, out_specs=out_specs, check_vma=False)
```

profile of v0, /device:TPU:0, one launch (start us, length us, event | category | flops | bytes accessed | tf_op | source)
XLA Modules:
  0.0 47.5 jit_solution(13307700867137716764)
XLA Ops:
  0.6 45.0 %shard_map.94 = (f32[16,1024]{1,0:T(8,128)S(1)}, f32[16,1024]{1,0:T(8,128)S(1)}, f32[5,4,16]{2,1,0:T(4,128)S(1)}) custom-call(s32[4,8]{1,0:T(4,128)} %columns_hbm.1, s32[4]{0:T(128)} %counts_hbm.1, f32[1,1024]{1,0:T(1,128)} %bitcast.5, s32[1,1024]{1,0:T(1,128)} %bitcast.6, s32[1,1024]{1,0:T(1,128)} %bitcast.7, f32[16,1024]{1,0:T(8,128)} %right_hbm.1, ...), custom_call_target="tpu_custom_call" | custom-call | tf_op jit(solution)/shard_map/pallas_call | solution.py:412
  45.6 0.6 %copy.13 = f32[16,1024]{1,0:T(8,128)} copy(f32[16,1024]{1,0:T(8,128)S(1)} %get-tuple-element.9) | data formatting | bytes 131072
  46.3 0.6 %copy.15 = f32[16,5,4]{0,2,1:T(4,128)} copy(f32[16,5,4]{0,2,1:T(4,128)S(1)} %bitcast.4) | data formatting | bytes 2560
  46.9 0.6 %copy.14 = f32[16,1024]{1,0:T(8,128)} copy(f32[16,1024]{1,0:T(8,128)S(1)} %get-tuple-element.10) | data formatting | bytes 131072
where the time goes:
time: 47.7 us; the launch traced here: 47.5 us
  Pallas kernels  45 us (94%)
  local copies, waits for them, and re-layouts  1.86 us (4%)
  between operations  0.64 us (1%)
    pallas_call x1, Pallas kernels, local(): pl.pallas_call(functools.partial(kernel, rows, cols, scaling), out_shape=...  45 us
    unnamed x3, local copies, waits for them, and re-layouts  1.86 us

commit v1 on v0

v1 whole, which is shorter than its diff:
```python
import functools
import math

import jax
import jax.numpy as jnp
from jax import lax
from jax.experimental import pallas as pl
from jax.experimental.pallas import tpu as pltpu
from jax.sharding import PartitionSpec as P

SKETCH = 1024
ITERS = 4
SHIFT = 1.75
epsilon = 1e-06
MESH = pl.DeviceIdType.MESH
f32 = jnp.float32
bf16 = jnp.bfloat16


def split_parts(value):
    head = value.astype(bf16)
    return jnp.concatenate([head, (value - head.astype(f32)).astype(bf16)], axis=0)


def extend_factor(factor, inverse, entries):
    row = len(inverse)
    for column in range(row):
        entry = entries[column]
        for inner in range(column):
            entry = entry - factor[row, inner] * factor[column, inner]
        factor[row, column] = entry * inverse[column]
    diag_part = entries[row]
    for inner in range(row):
        diag_part = diag_part - factor[row, inner] * factor[row, inner]
    inverse.append(lax.rsqrt(diag_part))


def factor_solve(factor, inverse, target):
    order = len(target)
    forward = []
    for column in range(order):
        entry = target[column]
        for inner in range(column):
            entry = entry - factor[column, inner] * forward[inner]
        forward.append(entry * inverse[column])
    result = [None] * order
    for column in reversed(range(order)):
        entry = forward[column]
        for inner in range(column + 1, order):
            entry = entry - factor[inner, column] * result[inner]
        result[column] = entry * inverse[column]
    return result


def nn_dot(a, b):
    return lax.dot_general(a, b, (((1,), (0,)), ((), ())), preferred_element_type=f32)


def kernel(
    rows,
    cols,
    scaling,
    columns_hbm,
    counts_hbm,
    diag_hbm,
    rows_hbm,
    signs_hbm,
    right_hbm,
    tiles_hbm,
    solution_ref,
    last_ref,
    hess_ref,
    columns_ref,
    counts_ref,
    diag_ref,
    rows_ref,
    signs_ref,
    tiles,
    band,
    index_ref,
    projector,
    krylov,
    window,
    part,
    land1,
    land2,
    grams,
    load_sem,
    tile_sem,
    halo_send,
    halo_recv,
    send1,
    recv1,
    send2,
    recv2,
    send3,
    recv3,
):
    row = lax.axis_index("row")
    col = lax.axis_index("col")
    devices = rows * cols
    me = row * cols + col
    block_rows, slots, tile, _ = tiles_hbm.shape
    span = 2 * block_rows + 1
    systems, width = right_hbm.shape
    all_blocks = block_rows * devices
    share = SKETCH // cols
    right = lax.rem(me + 1, devices)
    left = lax.rem(me + devices - 1, devices)
    right = (lax.div(right, cols), lax.rem(right, cols))
    left = (lax.div(left, cols), lax.rem(left, cols))
    col_to = [lax.rem(col + off, cols) for off in range(cols)]
    col_from = [lax.rem(col + cols - off, cols) for off in range(cols)]
    row_to = [lax.rem(row + off, rows) for off in range(rows)]
    row_from = [lax.rem(row + rows - off, rows) for off in range(rows)]

    barrier = pltpu.get_barrier_semaphore()
    for peer in (left, right):
        pl.semaphore_signal(barrier, inc=1, device_id=peer, device_id_type=MESH)
    for off in range(1, rows):
        pl.semaphore_signal(barrier, inc=1, device_id=(row_to[off], col), device_id_type=MESH)
    for off in range(1, cols):
        pl.semaphore_signal(barrier, inc=1, device_id=(row, col_to[off]), device_id_type=MESH)

    loads = [
        pltpu.make_async_copy(source, target, load_sem.at[n])
        for n, (source, target) in enumerate(
            [
                (rows_hbm, rows_ref),
                (signs_hbm, signs_ref),
                (columns_hbm, columns_ref),
                (counts_hbm, counts_ref),
                (diag_hbm, diag_ref),
            ]
            + [
                (right_hbm.at[:, pl.ds(b * tile, tile)], krylov.at[0, b])
                for b in range(block_rows)
            ]
        )
    ]
    tile_loads = [
        pltpu.make_async_copy(tiles_hbm.at[b], tiles.at[pl.ds(b * slots, slots)], tile_sem.at[b])
        for b in range(block_rows)
    ]
    for load in loads + tile_loads:
        load.start()
    tiles[block_rows * slots] = jnp.zeros((tile, tile), bf16)

    def halo_copies(k, b):
        return [
            pltpu.make_async_remote_copy(
                src_ref=window.at[k, block_rows + b],
                dst_ref=window.at[k, 2 * side * block_rows + b],
                send_sem=halo_send.at[k, side, b],
                recv_sem=halo_recv.at[k, side, b],
                device_id=peer,
                device_id_type=MESH,
            )
            for side, peer in ((0, right), (1, left))
        ]

    def copy1(k, off, block):
        return pltpu.make_async_remote_copy(
            src_ref=part.at[k, block],
            dst_ref=land1.at[k, off - 1],
            send_sem=send1.at[k, off - 1],
            recv_sem=recv1.at[k, off - 1],
            device_id=(row, col_to[off]),
            device_id_type=MESH,
        )

    def copy2(k, off, source):
        return pltpu.make_async_remote_copy(
            src_ref=land2.at[k, source],
            dst_ref=land2.at[k, source],
            send_sem=send2.at[k, off - 1],
            recv_sem=recv2.at[k, off - 1],
            device_id=(row_to[off], col),
            device_id_type=MESH,
        )

    def copy3(g, off, source):
        return pltpu.make_async_remote_copy(
            src_ref=grams.at[g, source],
            dst_ref=grams.at[g, source],
            send_sem=send3.at[g, off - 1],
            recv_sem=recv3.at[g, off - 1],
            device_id=(row, col_to[off]),
            device_id_type=MESH,
        )

    for load in loads[4:]:
        load.wait()
    for b in range(block_rows):
        window[0, block_rows + b] = split_parts(krylov[0, b])
    pl.semaphore_wait(barrier, rows + cols)
    for b in range(block_rows):
        for copy in halo_copies(0, b):
            copy.start()

    for load in loads[:4]:
        load.wait()
    first = me * block_rows
    for b in range(block_rows):
        spots = []
        for slot in range(slots):
            spot = lax.rem(columns_ref[b, slot] - first - b + block_rows + all_blocks, all_blocks)
            spots.append(jnp.where(slot < counts_ref[b], spot, span))
        for d in range(span):
            chosen = block_rows * slots
            for slot in range(slots):
                chosen = jnp.where(spots[slot] == d, b * slots + slot, chosen)
            index_ref[b * span + d] = chosen

    lanes = 128
    for c in range(width // lanes):
        here = pl.ds(c * lanes, lanes)
        target = jnp.broadcast_to(rows_ref[0:1, here].astype(f32), (lanes, lanes)).T
        sign = jnp.broadcast_to((2 * signs_ref[0:1, here] - 1).astype(f32), (lanes, lanes)).T
        for m in range(SKETCH // lanes):
            spot = (lax.broadcasted_iota(jnp.int32, (lanes, lanes), 1) + m * lanes).astype(f32)
            projector[here, pl.ds(m * lanes, lanes)] = jnp.where(spot == target, sign, 0.0).astype(bf16)

    for load in tile_loads:
        load.wait()

    def turn(i, carry):
        band[i] = tiles[index_ref[i]].T
        return carry

    lax.fori_loop(0, block_rows * span, turn, 0)

    def fold(total):
        return total[:systems] + total[systems:]

    def matvec(k, b, spots):
        total = None
        for spot in spots:
            if 0 <= spot - b < span:
                term = nn_dot(window[k, spot], band[b * span + spot - b])
                total = term if total is None else total + term
        return fold(total)

    own = list(range(block_rows, 2 * block_rows))
    outer = list(range(block_rows)) + list(range(2 * block_rows, 3 * block_rows))

    def stage1(k, values):
        for block in range(cols):
            total = None
            for b in range(block_rows):
                term = nn_dot(
                    values[b], projector[pl.ds(b * tile, tile), pl.ds(block * share, share)]
                )
                total = term if total is None else total + term
            part[k, block] = fold(total) * scaling
        for off in range(1, cols):
            copy1(k, off, col_to[off]).start()

    def stage2(k):
        for off in range(1, cols):
            copy1(k, off, 0).wait_recv()
        total = part[k, col]
        for off in range(1, cols):
            total = total + land1[k, off - 1]
        land2[k, row] = total
        for off in range(1, rows):
            copy2(k, off, row).start()

    def gathered(k):
        for off in range(1, rows):
            copy2(k, off, row_from[off]).wait_recv()
        total = land2[k, 0]
        for r in range(1, rows):
            total = total + land2[k, r]
        return total

    for k in range(ITERS):
        for b in range(block_rows):
            diag_b = diag_ref[0:1, pl.ds(b * tile, tile)] - SHIFT
            krylov[k + 1, b] = diag_b * krylov[k, b] + matvec(k, b, own)
        stage1(k, [window[k, block_rows + b] for b in range(block_rows)])
        if k >= 1:
            stage2(k - 1)
        for b in range(block_rows):
            for copy in halo_copies(k, b):
                copy.wait_recv()
        values = []
        for b in range(block_rows):
            fresh = krylov[k + 1, b] + matvec(k, b, outer)
            krylov[k + 1, b] = fresh
            values.append(split_parts(fresh))
            if k + 1 < ITERS:
                window[k + 1, block_rows + b] = values[b]
                for copy in halo_copies(k + 1, b):
                    copy.start()
    stage1(ITERS, values)
    stage2(ITERS - 1)

    lane = lax.broadcasted_iota(jnp.int32, (systems, lanes), 1)
    sketches = []

    def pair_sums(pairs):
        packed = jnp.zeros((systems, lanes), f32)
        for p, (i, j) in enumerate(pairs):
            value = jnp.sum(sketches[i] * sketches[j], axis=1, keepdims=True)
            packed = jnp.where(lane == p, value, packed)
        return packed

    def publish(g, packed):
        grams[g, col] = packed
        for off in range(1, cols):
            copy3(g, off, col).start()

    def collect(g, pairs, gram):
        for off in range(1, cols):
            copy3(g, off, col_from[off]).wait_recv()
        total = grams[g, 0]
        for c in range(1, cols):
            total = total + grams[g, c]
        for p, pair in enumerate(pairs):
            gram[pair] = jnp.broadcast_to(total[:, p : p + 1], (systems, lanes))

    early = [(i, j) for i in range(ITERS) for j in range(i + 1)]
    late = [(ITERS, j) for j in range(ITERS + 1)]
    for k in range(ITERS - 1):
        sketches.append(gathered(k))
    stage2(ITERS)
    sketches.append(gathered(ITERS - 1))
    publish(0, pair_sums(early))
    sketches.append(gathered(ITERS))
    publish(1, pair_sums(late))

    gram = {}
    lower = {}
    upright = []
    coords = []
    lengths = []
    hess = {}
    normal, normal_inverse = {}, []

    def lower_row(i):
        for j in range(i + 1):
            entry = gram[i, j]
            for m in range(j):
                entry = entry - lower[i, m] * lower[j, m]
            if j < i:
                lower[i, j] = entry * upright[j]
            else:
                upright.append(lax.rsqrt(entry))
                lower[i, i] = entry * upright[i]

    def arnoldi(j):
        image = [SHIFT * entry for entry in coords[j - 1]] + [coords[j - 1][j - 1]]
        for m in range(1, j):
            image[m] = image[m] + coords[j - 1][m - 1]
        fresh = image
        for i in range(j):
            seen = image[i] * lower[i, i]
            for m in range(i + 1, j + 1):
                seen = seen + image[m] * lower[m, i]
            coeff = seen * lengths[i]
            hess[i, j - 1] = coeff
            fresh = [
                entry - coeff * coords[i][m] if m <= i else entry for m, entry in enumerate(fresh)
            ]
        length = image[j] * lower[j, j]
        square = length * length + epsilon
        scale = lax.rsqrt(square)
        hess[j, j - 1] = square * scale
        coords.append([entry * scale for entry in fresh])
        lengths.append(1.0 / (length * scale))
        entries = []
        for n in range(j):
            entry = None
            for i in range(n + 2):
                term = hess[i, j - 1] * hess[i, n]
                entry = term if entry is None else entry + term
            entries.append(entry)
        extend_factor(normal, normal_inverse, entries)

    collect(0, early, gram)
    for i in range(ITERS):
        lower_row(i)
    square = gram[0, 0] + epsilon
    scale = lax.rsqrt(square)
    beta = square * scale
    coords.append([scale])
    lengths.append(1.0 / (lower[0, 0] * scale))
    for j in range(1, ITERS):
        arnoldi(j)
    collect(1, late, gram)
    lower_row(ITERS)
    arnoldi(ITERS)

    packed = jnp.zeros((systems, lanes), f32)
    for (i, j), value in hess.items():
        packed = jnp.where(lane == i * ITERS + j, value, packed)
    turned = packed.T
    for i in range(ITERS + 1):
        hess_ref[i] = turned[i * ITERS : (i + 1) * ITERS, :]

    weights = factor_solve(normal, normal_inverse, [beta * hess[0, n] for n in range(ITERS)])
    mixed = []
    for m in range(ITERS):
        entry = None
        for i in range(m, ITERS):
            term = weights[i] * coords[i][m]
            entry = term if entry is None else entry + term
        mixed.append(entry)

    def combine(target, factors, b):
        for c in range(tile // lanes):
            out = None
            for m, factor in enumerate(factors):
                term = factor * krylov[m, b, :, pl.ds(c * lanes, lanes)]
                out = term if out is None else out + term
            target[:, pl.ds(b * tile + c * lanes, lanes)] = out

    for b in range(block_rows):
        combine(last_ref, coords[ITERS], b)
        combine(solution_ref, mixed, b)

    for k in range(ITERS + 1):
        if k < ITERS:
            for b in range(block_rows):
                for copy in halo_copies(k, b):
                    copy.wait_send()
        for off in range(1, cols):
            copy1(k, off, col_to[off]).wait_send()
        for off in range(1, rows):
            copy2(k, off, row).wait_send()
    for g in range(2):
        for off in range(1, cols):
            copy3(g, off, col).wait_send()


def local(
    rows, cols, tile_values, block_columns, tile_counts, diagonal, sketch_rows, sketch_signs, right_side
):
    block_rows, slots, tile, _ = tile_values.shape
    span = 2 * block_rows + 1
    systems, width = right_side.shape
    scaling = 1.0 / math.sqrt(width * rows * cols)
    share = SKETCH // cols
    vectors = ITERS + 1
    vmem = pl.BlockSpec(memory_space=pltpu.VMEM)
    hbm = pl.BlockSpec(memory_space=pltpu.HBM)
    dma = pltpu.SemaphoreType.DMA
    iterate, last, hessenberg = pl.pallas_call(
        functools.partial(kernel, rows, cols, scaling),
        out_shape=(
            pltpu.VMEM((systems, width), f32),
            pltpu.VMEM((systems, width), f32),
            pltpu.VMEM((ITERS + 1, ITERS, systems), f32),
        ),
        in_specs=[hbm] * 7,
        out_specs=(vmem, vmem, vmem),
        scratch_shapes=[
            pltpu.SMEM(block_columns.shape, jnp.int32),
            pltpu.SMEM(tile_counts.shape, jnp.int32),
            pltpu.VMEM((1, width), f32),
            pltpu.VMEM((1, width), jnp.int32),
            pltpu.VMEM((1, width), jnp.int32),
            pltpu.VMEM((block_rows * slots + 1, tile, tile), bf16),
            pltpu.VMEM((block_rows * span, tile, tile), bf16),
            pltpu.SMEM((block_rows * span,), jnp.int32),
            pltpu.VMEM((width, SKETCH), bf16),
            pltpu.VMEM((vectors, block_rows, systems, tile), f32),
            pltpu.VMEM((ITERS, 3 * block_rows, 2 * systems, tile), bf16),
            pltpu.VMEM((vectors, cols, systems, share), f32),
            pltpu.VMEM((vectors, cols - 1, systems, share), f32),
            pltpu.VMEM((vectors, rows, systems, share), f32),
            pltpu.VMEM((2, cols, systems, 128), f32),
            dma((block_rows + 5,)),
            dma((block_rows,)),
            dma((ITERS, 2, block_rows)),
            dma((ITERS, 2, block_rows)),
            dma((vectors, cols - 1)),
            dma((vectors, cols - 1)),
            dma((vectors, rows - 1)),
            dma((vectors, rows - 1)),
            dma((2, cols - 1)),
            dma((2, cols - 1)),
        ],
        compiler_params=pltpu.CompilerParams(
            collective_id=0, has_side_effects=True, vmem_limit_bytes=67043328 - 160 * 1024
        ),
    )(
        block_columns,
        tile_counts,
        diagonal.reshape(1, width),
        sketch_rows.reshape(1, width),
        sketch_signs.reshape(1, width),
        right_side,
        tile_values,
    )
    return iterate, last, jnp.transpose(hessenberg, (2, 0, 1))


def solution(mesh):
    spec = P(("row", "col"))
    in_specs = (
        P(("row", "col"), None, None, None),
        P(("row", "col"), None),
        spec,
        spec,
        spec,
        spec,
        P(None, ("row", "col")),
    )
    out_specs = (P(None, ("row", "col")), P(None, ("row", "col")), P())
    body = functools.partial(local, mesh.shape["row"], mesh.shape["col"])
    return jax.shard_map(body, mesh=mesh, in_specs=in_specs, out_specs=out_specs, check_vma=False)
```

time: 47.7 us -> 41 us (0.86)
  Pallas kernels: 45 us -> 38.4 us
    pallas_call x1, Pallas kernels: 45 us -> 38.4 us  [local(): pl.pallas_call(functools.partial(kernel, rows, cols, scaling), out_shape=...]
where the time goes in v1:
time: 41 us; the launch traced here: 40.9 us
  Pallas kernels  38.4 us (94%)
  local copies, waits for them, and re-layouts  1.86 us (5%)
  between operations  0.64 us (2%)
    pallas_call x1, Pallas kernels, local(): pl.pallas_call(functools.partial(kernel, rows, cols, scaling), out_shape=...  38.4 us
    unnamed x3, local copies, waits for them, and re-layouts  1.86 us

profile of v1, /device:TPU:0, one launch (start us, length us, event | category | flops | bytes accessed | tf_op | source)
XLA Modules:
  0.0 40.9 jit_solution(15055262148807802254)
XLA Ops:
  0.6 38.4 %shard_map.94 = (f32[16,1024]{1,0:T(8,128)S(1)}, f32[16,1024]{1,0:T(8,128)S(1)}, f32[5,4,16]{2,1,0:T(4,128)S(1)}) custom-call(s32[4,8]{1,0:T(4,128)} %columns_hbm.1, s32[4]{0:T(128)} %counts_hbm.1, f32[1,1024]{1,0:T(1,128)} %bitcast.5, s32[1,1024]{1,0:T(1,128)} %bitcast.6, s32[1,1024]{1,0:T(1,128)} %bitcast.7, f32[16,1024]{1,0:T(8,128)} %right_hbm.1, ...), custom_call_target="tpu_custom_call" | custom-call | tf_op jit(solution)/shard_map/pallas_call | solution.py:449
  39.0 0.6 %copy.13 = f32[16,1024]{1,0:T(8,128)} copy(f32[16,1024]{1,0:T(8,128)S(1)} %get-tuple-element.9) | data formatting | bytes 131072
  39.6 0.6 %copy.15 = f32[16,5,4]{0,2,1:T(4,128)} copy(f32[16,5,4]{0,2,1:T(4,128)S(1)} %bitcast.4) | data formatting | bytes 2560
  40.2 0.6 %copy.14 = f32[16,1024]{1,0:T(8,128)} copy(f32[16,1024]{1,0:T(8,128)S(1)} %get-tuple-element.10) | data formatting | bytes 131072

commit v2 on v1

--- a/solution.py
+++ b/solution.py
@@ -104,26 +104,43 @@
     span = 2 * block_rows + 1
     systems, width = right_hbm.shape
     all_blocks = block_rows * devices
-    share = SKETCH // cols
+    share = land1.shape[-1]
+    team = SKETCH // share
+    mates = team // cols
+    chains = rows // mates
     right = lax.rem(me + 1, devices)
     left = lax.rem(me + devices - 1, devices)
     right = (lax.div(right, cols), lax.rem(right, cols))
     left = (lax.div(left, cols), lax.rem(left, cols))
-    col_to = [lax.rem(col + off, cols) for off in range(cols)]
-    col_from = [lax.rem(col + cols - off, cols) for off in range(cols)]
-    row_to = [lax.rem(row + off, rows) for off in range(rows)]
-    row_from = [lax.rem(row + rows - off, rows) for off in range(rows)]
-
+    chain = lax.div(row, mates)
+    seat = lax.rem(row, mates) * cols + col
+
+    def mate(number):
+        return (chain * mates + lax.div(number, cols), lax.rem(number, cols))
+
+    def link(number):
+        return (number * mates + lax.rem(row, mates), col)
+
+    parity = lax.rem(seat, 2)
+    pair_to = [lax.rem(lax.div(seat, 2) + turn, team // 2) for turn in range(team // 2)]
+    sides = [(turn, side) for turn in range(1, team // 2) for side in range(2)] + [(0, 1 - parity)]
+    seat_to = [lax.rem(seat + off, team) for off in range(team)]
+    seat_from = [lax.rem(seat + team - off, team) for off in range(team)]
+    chain_to = [lax.rem(chain + off, chains) for off in range(chains)]
+    chain_from = [lax.rem(chain + chains - off, chains) for off in range(chains)]
+
+    right_load = pltpu.make_async_copy(right_hbm, krylov.at[0], load_sem.at[0])
+    right_load.start()
     barrier = pltpu.get_barrier_semaphore()
     for peer in (left, right):
         pl.semaphore_signal(barrier, inc=1, device_id=peer, device_id_type=MESH)
-    for off in range(1, rows):
-        pl.semaphore_signal(barrier, inc=1, device_id=(row_to[off], col), device_id_type=MESH)
-    for off in range(1, cols):
-        pl.semaphore_signal(barrier, inc=1, device_id=(row, col_to[off]), device_id_type=MESH)
+    for number in chain_to[1:]:
+        pl.semaphore_signal(barrier, inc=1, device_id=link(number), device_id_type=MESH)
+    for number in seat_to[1:]:
+        pl.semaphore_signal(barrier, inc=1, device_id=mate(number), device_id_type=MESH)
 
     loads = [
-        pltpu.make_async_copy(source, target, load_sem.at[n])
+        pltpu.make_async_copy(source, target, load_sem.at[n + 1])
         for n, (source, target) in enumerate(
             [
                 (rows_hbm, rows_ref),
@@ -131,10 +148,6 @@
                 (columns_hbm, columns_ref),
                 (counts_hbm, counts_ref),
                 (diag_hbm, diag_ref),
-            ]
-            + [
-                (right_hbm.at[:, pl.ds(b * tile, tile)], krylov.at[0, b])
-                for b in range(block_rows)
             ]
         )
     ]
@@ -145,27 +158,49 @@
     for load in loads + tile_loads:
         load.start()
     tiles[block_rows * slots] = jnp.zeros((tile, tile), bf16)
-
-    def halo_copies(k, b):
+    half = block_rows // 2
+    lanes = 128
+
+    def block_at(b):
+        return pl.ds(b * tile, tile)
+
+    def halo_copies(k, far):
+        lower, upper = 0, block_rows - half
+        starts = ((0, right, lower if far else upper), (2, left, upper if far else lower))
         return [
             pltpu.make_async_remote_copy(
-                src_ref=window.at[k, block_rows + b],
-                dst_ref=window.at[k, 2 * side * block_rows + b],
-                send_sem=halo_send.at[k, side, b],
-                recv_sem=halo_recv.at[k, side, b],
+                src_ref=window.at[k, pl.ds(block_rows + start, half)],
+                dst_ref=window.at[k, pl.ds(side * block_rows + start, half)],
+                send_sem=halo_send.at[k, side // 2, far],
+                recv_sem=halo_recv.at[k, side // 2, far],
                 device_id=peer,
                 device_id_type=MESH,
             )
-            for side, peer in ((0, right), (1, left))
+            for side, peer, start in starts
         ]
 
-    def copy1(k, off, block):
+    def send_halo(k):
+        for far in range(2):
+            for copy in halo_copies(k, far):
+                copy.start()
+
+    def copy1(k, turn, side):
         return pltpu.make_async_remote_copy(
-            src_ref=part.at[k, block],
-            dst_ref=land1.at[k, off - 1],
-            send_sem=send1.at[k, off - 1],
-            recv_sem=recv1.at[k, off - 1],
-            device_id=(row, col_to[off]),
+            src_ref=part.at[k, 2 * turn + side],
+            dst_ref=land1.at[k, 2 * turn + parity],
+            send_sem=send1.at[k, 2 * turn + side],
+            recv_sem=recv1.at[k, 2 * turn + parity],
+            device_id=mate(2 * pair_to[turn] + side),
+            device_id_type=MESH,
+        )
+
+    def arrival1(k, turn, side):
+        return pltpu.make_async_remote_copy(
+            src_ref=part.at[k, 2 * turn + side],
+            dst_ref=land1.at[k, 2 * turn + side],
+            send_sem=send1.at[k, 2 * turn + side],
+            recv_sem=recv1.at[k, 2 * turn + side],
+            device_id=mate(2 * pair_to[turn] + side),
             device_id_type=MESH,
         )
 
@@ -175,7 +210,7 @@
             dst_ref=land2.at[k, source],
             send_sem=send2.at[k, off - 1],
             recv_sem=recv2.at[k, off - 1],
-            device_id=(row_to[off], col),
+            device_id=link(chain_to[off]),
             device_id_type=MESH,
         )
 
@@ -185,20 +220,17 @@
             dst_ref=grams.at[g, source],
             send_sem=send3.at[g, off - 1],
             recv_sem=recv3.at[g, off - 1],
-            device_id=(row, col_to[off]),
+            device_id=mate(seat_to[off]),
             device_id_type=MESH,
         )
 
-    for load in loads[4:]:
-        load.wait()
+    right_load.wait()
     for b in range(block_rows):
-        window[0, block_rows + b] = split_parts(krylov[0, b])
-    pl.semaphore_wait(barrier, rows + cols)
-    for b in range(block_rows):
-        for copy in halo_copies(0, b):
-            copy.start()
-
-    for load in loads[:4]:
+        window[0, block_rows + b] = split_parts(krylov[0, :, block_at(b)])
+    pl.semaphore_wait(barrier, team + chains)
+    send_halo(0)
+
+    for load in loads:
         load.wait()
     first = me * block_rows
     for b in range(block_rows):
@@ -212,7 +244,6 @@
                 chosen = jnp.where(spots[slot] == d, b * slots + slot, chosen)
             index_ref[b * span + d] = chosen
 
-    lanes = 128
     for c in range(width // lanes):
         here = pl.ds(c * lanes, lanes)
         target = jnp.broadcast_to(rows_ref[0:1, here].astype(f32), (lanes, lanes)).T
@@ -224,11 +255,12 @@
     for load in tile_loads:
         load.wait()
 
-    def turn(i, carry):
-        band[i] = tiles[index_ref[i]].T
+    def turn(b, carry):
+        for d in range(span):
+            band[b * span + d] = tiles[index_ref[b * span + d]].T
         return carry
 
-    lax.fori_loop(0, block_rows * span, turn, 0)
+    lax.fori_loop(0, block_rows, turn, 0)
 
     def fold(total):
         return total[:systems] + total[systems:]
@@ -241,60 +273,76 @@
                 total = term if total is None else total + term
         return fold(total)
 
-    own = list(range(block_rows, 2 * block_rows))
-    outer = list(range(block_rows)) + list(range(2 * block_rows, 3 * block_rows))
+    spots = list(range(3 * block_rows))
+    own = spots[block_rows : 2 * block_rows]
+    near = spots[half:block_rows] + spots[2 * block_rows : 2 * block_rows + half]
+    far = spots[:half] + spots[2 * block_rows + half :]
 
     def stage1(k, values):
-        for block in range(cols):
+        for turn in list(range(1, team // 2)) + [0]:
+            here = pl.ds(pl.multiple_of(pair_to[turn] * 2 * share, 2 * share), 2 * share)
             total = None
             for b in range(block_rows):
-                term = nn_dot(
-                    values[b], projector[pl.ds(b * tile, tile), pl.ds(block * share, share)]
-                )
+                term = nn_dot(values[b], projector[block_at(b), here])
                 total = term if total is None else total + term
-            part[k, block] = fold(total) * scaling
-        for off in range(1, cols):
-            copy1(k, off, col_to[off]).start()
+            total = fold(total) * scaling
+            for side in range(2):
+                part[k, 2 * turn + side] = total[:, side * share : (side + 1) * share]
+            for side in range(2) if turn > 0 else [1 - parity]:
+                copy1(k, turn, side).start()
 
     def stage2(k):
-        for off in range(1, cols):
-            copy1(k, off, 0).wait_recv()
-        total = part[k, col]
-        for off in range(1, cols):
-            total = total + land1[k, off - 1]
-        land2[k, row] = total
-        for off in range(1, rows):
-            copy2(k, off, row).start()
+        for turn, side in sides:
+            arrival1(k, turn, side).wait_recv()
+        total = part[k, parity]
+        for turn, side in sides:
+            total = total + land1[k, 2 * turn + side]
+        land2[k, chain] = total
+        for off in range(1, chains):
+            copy2(k, off, chain).start()
 
     def gathered(k):
-        for off in range(1, rows):
-            copy2(k, off, row_from[off]).wait_recv()
+        for off in range(1, chains):
+            copy2(k, off, chain_from[off]).wait_recv()
         total = land2[k, 0]
-        for r in range(1, rows):
+        for r in range(1, chains):
             total = total + land2[k, r]
         return total
 
     for k in range(ITERS):
         for b in range(block_rows):
-            diag_b = diag_ref[0:1, pl.ds(b * tile, tile)] - SHIFT
-            krylov[k + 1, b] = diag_b * krylov[k, b] + matvec(k, b, own)
-        stage1(k, [window[k, block_rows + b] for b in range(block_rows)])
-        if k >= 1:
-            stage2(k - 1)
+            scaled = (diag_ref[0:1, block_at(b)] - SHIFT) * krylov[k, :, block_at(b)]
+            krylov[k + 1, :, block_at(b)] = scaled + matvec(k, b, own)
+        for m in range(0 if k == 1 else max(k, 1), k + 1):
+            stage1(m, [window[m, block_rows + b] for b in range(block_rows)])
+        for m in range(0 if k == 2 else max(k - 1, 1), k):
+            stage2(m)
+        for copy in halo_copies(k, 0):
+            copy.wait_recv()
         for b in range(block_rows):
-            for copy in halo_copies(k, b):
-                copy.wait_recv()
+            krylov[k + 1, :, block_at(b)] += matvec(k, b, near)
+        for copy in halo_copies(k, 1):
+            copy.wait_recv()
         values = []
         for b in range(block_rows):
-            fresh = krylov[k + 1, b] + matvec(k, b, outer)
-            krylov[k + 1, b] = fresh
+            fresh = krylov[k + 1, :, block_at(b)] + matvec(k, b, far)
+            krylov[k + 1, :, block_at(b)] = fresh
             values.append(split_parts(fresh))
             if k + 1 < ITERS:
                 window[k + 1, block_rows + b] = values[b]
-                for copy in halo_copies(k + 1, b):
-                    copy.start()
+        if k + 1 < ITERS:
+            send_halo(k + 1)
     stage1(ITERS, values)
     stage2(ITERS - 1)
+
+    def finish_sends(k):
+        for far in range(2 if k < ITERS else 0):
+            for copy in halo_copies(k, far):
+                copy.wait_send()
+        for turn, side in sides:
+            copy1(k, turn, side).wait_send()
+        for off in range(1, chains):
+            copy2(k, off, chain).wait_send()
 
     lane = lax.broadcasted_iota(jnp.int32, (systems, lanes), 1)
     sketches = []
@@ -307,15 +355,15 @@
         return packed
 
     def publish(g, packed):
-        grams[g, col] = packed
-        for off in range(1, cols):
-            copy3(g, off, col).start()
+        grams[g, seat] = packed
+        for off in range(1, team):
+            copy3(g, off, seat).start()
 
     def collect(g, pairs, gram):
-        for off in range(1, cols):
-            copy3(g, off, col_from[off]).wait_recv()
+        for off in range(1, team):
+            copy3(g, off, seat_from[off]).wait_recv()
         total = grams[g, 0]
-        for c in range(1, cols):
+        for c in range(1, team):
             total = total + grams[g, c]
         for p, pair in enumerate(pairs):
             gram[pair] = jnp.broadcast_to(total[:, p : p + 1], (systems, lanes))
@@ -327,6 +375,8 @@
     stage2(ITERS)
     sketches.append(gathered(ITERS - 1))
     publish(0, pair_sums(early))
+    for k in range(ITERS):
+        finish_sends(k)
     sketches.append(gathered(ITERS))
     publish(1, pair_sums(late))
 
@@ -412,7 +462,7 @@
         for c in range(tile // lanes):
             out = None
             for m, factor in enumerate(factors):
-                term = factor * krylov[m, b, :, pl.ds(c * lanes, lanes)]
+                term = factor * krylov[m, :, pl.ds(b * tile + c * lanes, lanes)]
                 out = term if out is None else out + term
             target[:, pl.ds(b * tile + c * lanes, lanes)] = out
 
@@ -420,18 +470,22 @@
         combine(last_ref, coords[ITERS], b)
         combine(solution_ref, mixed, b)
 
-    for k in range(ITERS + 1):
-        if k < ITERS:
-            for b in range(block_rows):
-                for copy in halo_copies(k, b):
-                    copy.wait_send()
-        for off in range(1, cols):
-            copy1(k, off, col_to[off]).wait_send()
-        for off in range(1, rows):
-            copy2(k, off, row).wait_send()
+    finish_sends(ITERS)
     for g in range(2):
-        for off in range(1, cols):
-            copy3(g, off, col).wait_send()
+        for off in range(1, team):
+            copy3(g, off, seat).wait_send()
+
+
+def deliver(*refs):
+    sources, targets, sem = refs[:3], refs[3:6], refs[6]
+    copies = [
+        pltpu.make_async_copy(source, target, sem.at[n])
+        for n, (source, target) in enumerate(zip(sources, targets))
+    ]
+    for copy in copies:
+        copy.start()
+    for copy in copies:
+        copy.wait()
 
 
 def local(
@@ -441,12 +495,15 @@
     span = 2 * block_rows + 1
     systems, width = right_side.shape
     scaling = 1.0 / math.sqrt(width * rows * cols)
-    share = SKETCH // cols
+    mates = 2 if rows % 2 == 0 else 1
+    team = mates * cols
+    chains = rows // mates
+    share = SKETCH // team
     vectors = ITERS + 1
     vmem = pl.BlockSpec(memory_space=pltpu.VMEM)
     hbm = pl.BlockSpec(memory_space=pltpu.HBM)
     dma = pltpu.SemaphoreType.DMA
-    iterate, last, hessenberg = pl.pallas_call(
+    found = pl.pallas_call(
         functools.partial(kernel, rows, cols, scaling),
         out_shape=(
             pltpu.VMEM((systems, width), f32),
@@ -465,22 +522,22 @@
             pltpu.VMEM((block_rows * span, tile, tile), bf16),
             pltpu.SMEM((block_rows * span,), jnp.int32),
             pltpu.VMEM((width, SKETCH), bf16),
-            pltpu.VMEM((vectors, block_rows, systems, tile), f32),
+            pltpu.VMEM((vectors, systems, width), f32),
             pltpu.VMEM((ITERS, 3 * block_rows, 2 * systems, tile), bf16),
-            pltpu.VMEM((vectors, cols, systems, share), f32),
-            pltpu.VMEM((vectors, cols - 1, systems, share), f32),
-            pltpu.VMEM((vectors, rows, systems, share), f32),
-            pltpu.VMEM((2, cols, systems, 128), f32),
-            dma((block_rows + 5,)),
+            pltpu.VMEM((vectors, team, systems, share), f32),
+            pltpu.VMEM((vectors, team, systems, share), f32),
+            pltpu.VMEM((vectors, chains, systems, share), f32),
+            pltpu.VMEM((2, team, systems, 128), f32),
+            dma((6,)),
             dma((block_rows,)),
-            dma((ITERS, 2, block_rows)),
-            dma((ITERS, 2, block_rows)),
-            dma((vectors, cols - 1)),
-            dma((vectors, cols - 1)),
-            dma((vectors, rows - 1)),
-            dma((vectors, rows - 1)),
-            dma((2, cols - 1)),
-            dma((2, cols - 1)),
+            dma((ITERS, 2, 2)),
+            dma((ITERS, 2, 2)),
+            dma((vectors, team)),
+            dma((vectors, team)),
+            dma((vectors, chains - 1)),
+            dma((vectors, chains - 1)),
+            dma((2, team - 1)),
+            dma((2, team - 1)),
         ],
         compiler_params=pltpu.CompilerParams(
             collective_id=0, has_side_effects=True, vmem_limit_bytes=67043328 - 160 * 1024
@@ -494,6 +551,13 @@
         right_side,
         tile_values,
     )
+    iterate, last, hessenberg = pl.pallas_call(
+        deliver,
+        out_shape=[jax.ShapeDtypeStruct(ref.shape, f32) for ref in found],
+        in_specs=[vmem] * 3,
+        out_specs=[hbm] * 3,
+        scratch_shapes=[dma((3,))],
+    )(*[pltpu.with_memory_space_constraint(ref, pltpu.VMEM) for ref in found])
     return iterate, last, jnp.transpose(hessenberg, (2, 0, 1))
 
 

time: 41 us -> 37.2 us (0.907)
  Pallas kernels: 38.4 us -> 36.4 us
  local copies, waits for them, and re-layouts: 1.86 us -> 0 us
    pallas_call x1, Pallas kernels: 38.4 us -> 35.7 us  [local(): pl.pallas_call(functools.partial(kernel, rows, cols, scaling), out_shape=...]
    unnamed x3 -> x0, local copies, waits for them, and re-layouts: 1.86 us -> none
    pallas_call x0 -> x1, Pallas kernels: none -> 0.68 us  [local(): pl.pallas_call(deliver, out_shape=[jax.ShapeDtypeStruct(ref.shape, f32) f...]
where the time goes in v2:
time: 37.2 us; the launch traced here: 37 us
  Pallas kernels  36.4 us (98%)
  between operations  0.64 us (2%)
    pallas_call x1, Pallas kernels, local(): pl.pallas_call(functools.partial(kernel, rows, cols, scaling), out_shape=...  35.7 us

profile of v2, /device:TPU:0, one launch (start us, length us, event | category | flops | bytes accessed | tf_op | source)
XLA Modules:
  0.0 37.0 jit_solution(9825459218612286689)
XLA Ops:
  0.6 35.7 %shard_map.94 = (f32[16,1024]{1,0:T(8,128)S(1)}, f32[16,1024]{1,0:T(8,128)S(1)}, f32[5,4,16]{2,1,0:T(4,128)S(1)}) custom-call(s32[4,8]{1,0:T(4,128)} %columns_hbm.1, s32[4]{0:T(128)} %counts_hbm.1, f32[1,1024]{1,0:T(1,128)} %bitcast.4, s32[1,1024]{1,0:T(1,128)} %bitcast.5, s32[1,1024]{1,0:T(1,128)} %bitcast.6, f32[16,1024]{1,0:T(8,128)} %right_hbm.1, ...), custom_call_target="tpu_custom_call" | custom-call | tf_op jit(solution)/shard_map/pallas_call | solution.py:506
  36.3 0.7 %shard_map.95 = (f32[16,1024]{1,0:T(8,128)}, f32[16,1024]{1,0:T(8,128)}, f32[5,4,16]{2,1,0:T(4,128)}) custom-call(f32[16,1024]{1,0:T(8,128)S(1)} %get-tuple-element.9.refs_0_, f32[16,1024]{1,0:T(8,128)S(1)} %get-tuple-element.10.refs_1_, f32[5,4,16]{2,1,0:T(4,128)S(1)} %get-tuple-element.11.refs_2_), custom_call_target="tpu_custom_call" | custom-call | tf_op jit(solution)/shard_map/pallas_call | solution.py:554

commit v3 on v2

--- a/solution.py
+++ b/solution.py
@@ -152,7 +152,7 @@
         )
     ]
     tile_loads = [
-        pltpu.make_async_copy(tiles_hbm.at[b], tiles.at[pl.ds(b * slots, slots)], tile_sem.at[b])
+        pltpu.make_async_copy(tiles_hbm.at[b], tiles.at[pl.ds(b * slots, slots)], tile_sem)
         for b in range(block_rows)
     ]
     for load in loads + tile_loads:
@@ -171,14 +171,27 @@
             pltpu.make_async_remote_copy(
                 src_ref=window.at[k, pl.ds(block_rows + start, half)],
                 dst_ref=window.at[k, pl.ds(side * block_rows + start, half)],
-                send_sem=halo_send.at[k, side // 2, far],
-                recv_sem=halo_recv.at[k, side // 2, far],
+                send_sem=halo_send,
+                recv_sem=halo_recv.at[k, far],
                 device_id=peer,
                 device_id_type=MESH,
             )
             for side, peer, start in starts
         ]
 
+    def whole(ref, send_sem, recv_sem):
+        return pltpu.make_async_remote_copy(
+            src_ref=ref,
+            dst_ref=ref,
+            send_sem=send_sem,
+            recv_sem=recv_sem,
+            device_id=right,
+            device_id_type=MESH,
+        )
+
+    def await_halo(k, far):
+        whole(window.at[k, pl.ds(0, 2 * half)], halo_send, halo_recv.at[k, far]).wait_recv()
+
     def send_halo(k):
         for far in range(2):
             for copy in halo_copies(k, far):
@@ -188,18 +201,8 @@
         return pltpu.make_async_remote_copy(
             src_ref=part.at[k, 2 * turn + side],
             dst_ref=land1.at[k, 2 * turn + parity],
-            send_sem=send1.at[k, 2 * turn + side],
-            recv_sem=recv1.at[k, 2 * turn + parity],
-            device_id=mate(2 * pair_to[turn] + side),
-            device_id_type=MESH,
-        )
-
-    def arrival1(k, turn, side):
-        return pltpu.make_async_remote_copy(
-            src_ref=part.at[k, 2 * turn + side],
-            dst_ref=land1.at[k, 2 * turn + side],
-            send_sem=send1.at[k, 2 * turn + side],
-            recv_sem=recv1.at[k, 2 * turn + side],
+            send_sem=send1,
+            recv_sem=recv1.at[k],
             device_id=mate(2 * pair_to[turn] + side),
             device_id_type=MESH,
         )
@@ -208,8 +211,8 @@
         return pltpu.make_async_remote_copy(
             src_ref=land2.at[k, source],
             dst_ref=land2.at[k, source],
-            send_sem=send2.at[k, off - 1],
-            recv_sem=recv2.at[k, off - 1],
+            send_sem=send2,
+            recv_sem=recv2.at[k],
             device_id=link(chain_to[off]),
             device_id_type=MESH,
         )
@@ -218,8 +221,8 @@
         return pltpu.make_async_remote_copy(
             src_ref=grams.at[g, source],
             dst_ref=grams.at[g, source],
-            send_sem=send3.at[g, off - 1],
-            recv_sem=recv3.at[g, off - 1],
+            send_sem=send3,
+            recv_sem=recv3.at[g],
             device_id=mate(seat_to[off]),
             device_id_type=MESH,
         )
@@ -252,8 +255,8 @@
             spot = (lax.broadcasted_iota(jnp.int32, (lanes, lanes), 1) + m * lanes).astype(f32)
             projector[here, pl.ds(m * lanes, lanes)] = jnp.where(spot == target, sign, 0.0).astype(bf16)
 
-    for load in tile_loads:
-        load.wait()
+    used = tiles.at[pl.ds(0, block_rows * slots)]
+    pltpu.make_async_copy(used, used, tile_sem).wait()
 
     def turn(b, carry):
         for d in range(span):
@@ -279,7 +282,7 @@
     far = spots[:half] + spots[2 * block_rows + half :]
 
     def stage1(k, values):
-        for turn in list(range(1, team // 2)) + [0]:
+        for turn in range(team // 2):
             here = pl.ds(pl.multiple_of(pair_to[turn] * 2 * share, 2 * share), 2 * share)
             total = None
             for b in range(block_rows):
@@ -288,12 +291,11 @@
             total = fold(total) * scaling
             for side in range(2):
                 part[k, 2 * turn + side] = total[:, side * share : (side + 1) * share]
-            for side in range(2) if turn > 0 else [1 - parity]:
-                copy1(k, turn, side).start()
+        for turn, side in sides:
+            copy1(k, turn, side).start()
 
     def stage2(k):
-        for turn, side in sides:
-            arrival1(k, turn, side).wait_recv()
+        whole(land1.at[k, pl.ds(0, team - 1)], send1, recv1.at[k]).wait_recv()
         total = part[k, parity]
         for turn, side in sides:
             total = total + land1[k, 2 * turn + side]
@@ -302,8 +304,7 @@
             copy2(k, off, chain).start()
 
     def gathered(k):
-        for off in range(1, chains):
-            copy2(k, off, chain_from[off]).wait_recv()
+        whole(land2.at[k, pl.ds(0, chains - 1)], send2, recv2.at[k]).wait_recv()
         total = land2[k, 0]
         for r in range(1, chains):
             total = total + land2[k, r]
@@ -317,12 +318,10 @@
             stage1(m, [window[m, block_rows + b] for b in range(block_rows)])
         for m in range(0 if k == 2 else max(k - 1, 1), k):
             stage2(m)
-        for copy in halo_copies(k, 0):
-            copy.wait_recv()
+        await_halo(k, 0)
         for b in range(block_rows):
             krylov[k + 1, :, block_at(b)] += matvec(k, b, near)
-        for copy in halo_copies(k, 1):
-            copy.wait_recv()
+        await_halo(k, 1)
         values = []
         for b in range(block_rows):
             fresh = krylov[k + 1, :, block_at(b)] + matvec(k, b, far)
@@ -335,15 +334,6 @@
     stage1(ITERS, values)
     stage2(ITERS - 1)
 
-    def finish_sends(k):
-        for far in range(2 if k < ITERS else 0):
-            for copy in halo_copies(k, far):
-                copy.wait_send()
-        for turn, side in sides:
-            copy1(k, turn, side).wait_send()
-        for off in range(1, chains):
-            copy2(k, off, chain).wait_send()
-
     lane = lax.broadcasted_iota(jnp.int32, (systems, lanes), 1)
     sketches = []
 
@@ -360,8 +350,7 @@
             copy3(g, off, seat).start()
 
     def collect(g, pairs, gram):
-        for off in range(1, team):
-            copy3(g, off, seat_from[off]).wait_recv()
+        whole(grams.at[g, pl.ds(0, team - 1)], send3, recv3.at[g]).wait_recv()
         total = grams[g, 0]
         for c in range(1, team):
             total = total + grams[g, c]
@@ -375,8 +364,6 @@
     stage2(ITERS)
     sketches.append(gathered(ITERS - 1))
     publish(0, pair_sums(early))
-    for k in range(ITERS):
-        finish_sends(k)
     sketches.append(gathered(ITERS))
     publish(1, pair_sums(late))
 
@@ -470,10 +457,10 @@
         combine(last_ref, coords[ITERS], b)
         combine(solution_ref, mixed, b)
 
-    finish_sends(ITERS)
-    for g in range(2):
-        for off in range(1, team):
-            copy3(g, off, seat).wait_send()
+    whole(window.at[:, pl.ds(0, 2 * block_rows)], halo_send, halo_recv.at[0, 0]).wait_send()
+    whole(part.at[:, pl.ds(0, team - 1)], send1, recv1.at[0]).wait_send()
+    whole(land2.at[:, pl.ds(0, chains - 1)], send2, recv2.at[0]).wait_send()
+    whole(grams.at[:, pl.ds(0, team - 1)], send3, recv3.at[0]).wait_send()
 
 
 def deliver(*refs):
@@ -529,15 +516,15 @@
             pltpu.VMEM((vectors, chains, systems, share), f32),
             pltpu.VMEM((2, team, systems, 128), f32),
             dma((6,)),
-            dma((block_rows,)),
-            dma((ITERS, 2, 2)),
-            dma((ITERS, 2, 2)),
-            dma((vectors, team)),
-            dma((vectors, team)),
-            dma((vectors, chains - 1)),
-            dma((vectors, chains - 1)),
-            dma((2, team - 1)),
-            dma((2, team - 1)),
+            dma,
+            dma,
+            dma((ITERS, 2)),
+            dma,
+            dma((vectors,)),
+            dma,
+            dma((vectors,)),
+            dma,
+            dma((2,)),
         ],
         compiler_params=pltpu.CompilerParams(
             collective_id=0, has_side_effects=True, vmem_limit_bytes=67043328 - 160 * 1024

time: 37.2 us -> 35.7 us (0.960)
  Pallas kernels: 36.4 us -> 34.6 us
    pallas_call x1, Pallas kernels: 35.7 us -> 33.9 us  [local(): pl.pallas_call(functools.partial(kernel, rows, cols, scaling), out_shape=...]
where the time goes in v3:
time: 35.7 us; the launch traced here: 35.3 us
  Pallas kernels  34.6 us (97%)
  between operations  0.64 us (2%)
    pallas_call x1, Pallas kernels, local(): pl.pallas_call(functools.partial(kernel, rows, cols, scaling), out_shape=...  33.9 us

profile of v3, /device:TPU:0, one launch (start us, length us, event | category | flops | bytes accessed | tf_op | source)
XLA Modules:
  0.0 35.3 jit_solution(7135471210215775249)
XLA Ops:
  0.6 33.9 %shard_map.94 = (f32[16,1024]{1,0:T(8,128)S(1)}, f32[16,1024]{1,0:T(8,128)S(1)}, f32[5,4,16]{2,1,0:T(4,128)S(1)}) custom-call(s32[4,8]{1,0:T(4,128)} %columns_hbm.1, s32[4]{0:T(128)} %counts_hbm.1, f32[1,1024]{1,0:T(1,128)} %bitcast.4, s32[1,1024]{1,0:T(1,128)} %bitcast.5, s32[1,1024]{1,0:T(1,128)} %bitcast.6, f32[16,1024]{1,0:T(8,128)} %right_hbm.1, ...), custom_call_target="tpu_custom_call" | custom-call | tf_op jit(solution)/shard_map/pallas_call | solution.py:493
  34.6 0.7 %shard_map.95 = (f32[16,1024]{1,0:T(8,128)}, f32[16,1024]{1,0:T(8,128)}, f32[5,4,16]{2,1,0:T(4,128)}) custom-call(f32[16,1024]{1,0:T(8,128)S(1)} %get-tuple-element.9.refs_0_, f32[16,1024]{1,0:T(8,128)S(1)} %get-tuple-element.10.refs_1_, f32[5,4,16]{2,1,0:T(4,128)S(1)} %get-tuple-element.11.refs_2_), custom_call_target="tpu_custom_call" | custom-call | tf_op jit(solution)/shard_map/pallas_call | solution.py:541

commit v4 on v3

--- a/solution.py
+++ b/solution.py
@@ -112,6 +112,11 @@
     left = lax.rem(me + devices - 1, devices)
     right = (lax.div(right, cols), lax.rem(right, cols))
     left = (lax.div(left, cols), lax.rem(left, cols))
+    barrier = pltpu.get_barrier_semaphore()
+    for peer in (left, right):
+        pl.semaphore_signal(barrier, inc=1, device_id=peer, device_id_type=MESH)
+    right_load = pltpu.make_async_copy(right_hbm, krylov.at[0], load_sem.at[0])
+    right_load.start()
     chain = lax.div(row, mates)
     seat = lax.rem(row, mates) * cols + col
 
@@ -125,20 +130,12 @@
     pair_to = [lax.rem(lax.div(seat, 2) + turn, team // 2) for turn in range(team // 2)]
     sides = [(turn, side) for turn in range(1, team // 2) for side in range(2)] + [(0, 1 - parity)]
     seat_to = [lax.rem(seat + off, team) for off in range(team)]
-    seat_from = [lax.rem(seat + team - off, team) for off in range(team)]
     chain_to = [lax.rem(chain + off, chains) for off in range(chains)]
-    chain_from = [lax.rem(chain + chains - off, chains) for off in range(chains)]
-
-    right_load = pltpu.make_async_copy(right_hbm, krylov.at[0], load_sem.at[0])
-    right_load.start()
-    barrier = pltpu.get_barrier_semaphore()
-    for peer in (left, right):
-        pl.semaphore_signal(barrier, inc=1, device_id=peer, device_id_type=MESH)
+
     for number in chain_to[1:]:
         pl.semaphore_signal(barrier, inc=1, device_id=link(number), device_id_type=MESH)
     for number in seat_to[1:]:
         pl.semaphore_signal(barrier, inc=1, device_id=mate(number), device_id_type=MESH)
-
     loads = [
         pltpu.make_async_copy(source, target, load_sem.at[n + 1])
         for n, (source, target) in enumerate(
@@ -164,19 +161,17 @@
     def block_at(b):
         return pl.ds(b * tile, tile)
 
-    def halo_copies(k, far):
-        lower, upper = 0, block_rows - half
-        starts = ((0, right, lower if far else upper), (2, left, upper if far else lower))
+    def halo_copies(k, start):
         return [
             pltpu.make_async_remote_copy(
                 src_ref=window.at[k, pl.ds(block_rows + start, half)],
                 dst_ref=window.at[k, pl.ds(side * block_rows + start, half)],
                 send_sem=halo_send,
-                recv_sem=halo_recv.at[k, far],
+                recv_sem=halo_recv.at[k, side // 2, start // half],
                 device_id=peer,
                 device_id_type=MESH,
             )
-            for side, peer, start in starts
+            for side, peer in ((0, right), (2, left))
         ]
 
     def whole(ref, send_sem, recv_sem):
@@ -189,13 +184,13 @@
             device_id_type=MESH,
         )
 
-    def await_halo(k, far):
-        whole(window.at[k, pl.ds(0, 2 * half)], halo_send, halo_recv.at[k, far]).wait_recv()
-
-    def send_halo(k):
-        for far in range(2):
-            for copy in halo_copies(k, far):
-                copy.start()
+    def await_halo(k, side, start):
+        spots = pl.ds(2 * side * block_rows + start, half)
+        whole(window.at[k, spots], halo_send, halo_recv.at[k, side, start // half]).wait_recv()
+
+    def send_halo(k, start):
+        for copy in halo_copies(k, start):
+            copy.start()
 
     def copy1(k, turn, side):
         return pltpu.make_async_remote_copy(
@@ -231,7 +226,8 @@
     for b in range(block_rows):
         window[0, block_rows + b] = split_parts(krylov[0, :, block_at(b)])
     pl.semaphore_wait(barrier, team + chains)
-    send_halo(0)
+    send_halo(0, 0)
+    send_halo(0, half)
 
     for load in loads:
         load.wait()
@@ -278,8 +274,47 @@
 
     spots = list(range(3 * block_rows))
     own = spots[block_rows : 2 * block_rows]
-    near = spots[half:block_rows] + spots[2 * block_rows : 2 * block_rows + half]
-    far = spots[:half] + spots[2 * block_rows + half :]
+    groups = ((0, range(half)), (half, range(half, block_rows)))
+
+    def add(k, side, starts, wanted):
+        for b in wanted:
+            here = [
+                spot
+                for start in starts
+                for spot in range(2 * side * block_rows + start, 2 * side * block_rows + start + half)
+                if 0 <= spot - b < span
+            ]
+            if here:
+                krylov[k + 1, :, block_at(b)] += matvec(k, b, here)
+
+    def publish_rows(k, start, wanted):
+        for b in wanted:
+            window[k + 1, block_rows + b] = split_parts(krylov[k + 1, :, block_at(b)])
+        if k + 1 < ITERS:
+            send_halo(k + 1, start)
+
+    def left_last(k):
+        for start in (0, half):
+            await_halo(k, 1, start)
+        add(k, 1, (0, half), range(block_rows))
+        await_halo(k, 0, 0)
+        add(k, 0, (0,), range(block_rows))
+        await_halo(k, 0, half)
+        for start, wanted in groups:
+            add(k, 0, (half,), wanted)
+            publish_rows(k, start, wanted)
+
+    def right_last(k):
+        for start in (0, half):
+            await_halo(k, 0, start)
+        add(k, 0, (0, half), range(block_rows))
+        await_halo(k, 1, 0)
+        add(k, 1, (0,), range(half))
+        publish_rows(k, 0, range(half))
+        add(k, 1, (0,), range(half, block_rows))
+        await_halo(k, 1, half)
+        add(k, 1, (half,), range(half, block_rows))
+        publish_rows(k, half, range(half, block_rows))
 
     def stage1(k, values):
         for turn in range(team // 2):
@@ -318,20 +353,9 @@
             stage1(m, [window[m, block_rows + b] for b in range(block_rows)])
         for m in range(0 if k == 2 else max(k - 1, 1), k):
             stage2(m)
-        await_halo(k, 0)
-        for b in range(block_rows):
-            krylov[k + 1, :, block_at(b)] += matvec(k, b, near)
-        await_halo(k, 1)
-        values = []
-        for b in range(block_rows):
-            fresh = krylov[k + 1, :, block_at(b)] + matvec(k, b, far)
-            krylov[k + 1, :, block_at(b)] = fresh
-            values.append(split_parts(fresh))
-            if k + 1 < ITERS:
-                window[k + 1, block_rows + b] = values[b]
-        if k + 1 < ITERS:
-            send_halo(k + 1)
-    stage1(ITERS, values)
+        pl.when(me < devices // 2)(functools.partial(left_last, k))
+        pl.when(me >= devices // 2)(functools.partial(right_last, k))
+    stage1(ITERS, [window[ITERS, block_rows + b] for b in range(block_rows)])
     stage2(ITERS - 1)
 
     lane = lax.broadcasted_iota(jnp.int32, (systems, lanes), 1)
@@ -457,7 +481,8 @@
         combine(last_ref, coords[ITERS], b)
         combine(solution_ref, mixed, b)
 
-    whole(window.at[:, pl.ds(0, 2 * block_rows)], halo_send, halo_recv.at[0, 0]).wait_send()
+    sent = window.at[pl.ds(0, ITERS), pl.ds(0, 2 * block_rows)]
+    whole(sent, halo_send, halo_recv.at[0, 0, 0]).wait_send()
     whole(part.at[:, pl.ds(0, team - 1)], send1, recv1.at[0]).wait_send()
     whole(land2.at[:, pl.ds(0, chains - 1)], send2, recv2.at[0]).wait_send()
     whole(grams.at[:, pl.ds(0, team - 1)], send3, recv3.at[0]).wait_send()
@@ -510,7 +535,7 @@
             pltpu.SMEM((block_rows * span,), jnp.int32),
             pltpu.VMEM((width, SKETCH), bf16),
             pltpu.VMEM((vectors, systems, width), f32),
-            pltpu.VMEM((ITERS, 3 * block_rows, 2 * systems, tile), bf16),
+            pltpu.VMEM((vectors, 3 * block_rows, 2 * systems, tile), bf16),
             pltpu.VMEM((vectors, team, systems, share), f32),
             pltpu.VMEM((vectors, team, systems, share), f32),
             pltpu.VMEM((vectors, chains, systems, share), f32),
@@ -518,7 +543,7 @@
             dma((6,)),
             dma,
             dma,
-            dma((ITERS, 2)),
+            dma((ITERS, 2, 2)),
             dma,
             dma((vectors,)),
             dma,

time: 35.7 us -> 35 us (0.980)
  Pallas kernels: 34.6 us -> 34.2 us
    pallas_call x1, Pallas kernels: 33.9 us -> 33.5 us  [local(): pl.pallas_call(functools.partial(kernel, rows, cols, scaling), out_shape=...]
where the time goes in v4:
time: 35 us; the launch traced here: 34.9 us
  Pallas kernels  34.2 us (98%)
  between operations  0.64 us (2%)
    pallas_call x1, Pallas kernels, local(): pl.pallas_call(functools.partial(kernel, rows, cols, scaling), out_shape=...  33.5 us

profile of v4, /device:TPU:0, one launch (start us, length us, event | category | flops | bytes accessed | tf_op | source)
XLA Modules:
  0.0 34.9 jit_solution(6025838739501427011)
XLA Ops:
  0.6 33.5 %shard_map.94 = (f32[16,1024]{1,0:T(8,128)S(1)}, f32[16,1024]{1,0:T(8,128)S(1)}, f32[5,4,16]{2,1,0:T(4,128)S(1)}) custom-call(s32[4,8]{1,0:T(4,128)} %columns_hbm.1, s32[4]{0:T(128)} %counts_hbm.1, f32[1,1024]{1,0:T(1,128)} %bitcast.4, s32[1,1024]{1,0:T(1,128)} %bitcast.5, s32[1,1024]{1,0:T(1,128)} %bitcast.6, f32[16,1024]{1,0:T(8,128)} %right_hbm.1, ...), custom_call_target="tpu_custom_call" | custom-call | tf_op jit(solution)/shard_map/pallas_call | solution.py:518
  34.2 0.7 %shard_map.95 = (f32[16,1024]{1,0:T(8,128)}, f32[16,1024]{1,0:T(8,128)}, f32[5,4,16]{2,1,0:T(4,128)}) custom-call(f32[16,1024]{1,0:T(8,128)S(1)} %get-tuple-element.9.refs_0_, f32[16,1024]{1,0:T(8,128)S(1)} %get-tuple-element.10.refs_1_, f32[5,4,16]{2,1,0:T(4,128)S(1)} %get-tuple-element.11.refs_2_), custom_call_target="tpu_custom_call" | custom-call | tf_op jit(solution)/shard_map/pallas_call | solution.py:566

commit v5 on v4

--- a/solution.py
+++ b/solution.py
@@ -84,6 +84,8 @@
     part,
     land1,
     land2,
+    direct,
+    straight,
     grams,
     load_sem,
     tile_sem,
@@ -95,6 +97,8 @@
     recv2,
     send3,
     recv3,
+    send4,
+    recv4,
 ):
     row = lax.axis_index("row")
     col = lax.axis_index("col")
@@ -136,6 +140,8 @@
         pl.semaphore_signal(barrier, inc=1, device_id=link(number), device_id_type=MESH)
     for number in seat_to[1:]:
         pl.semaphore_signal(barrier, inc=1, device_id=mate(number), device_id_type=MESH)
+    last = devices - 1
+    trailing = jnp.logical_or(me == 0, me == last)
     loads = [
         pltpu.make_async_copy(source, target, load_sem.at[n + 1])
         for n, (source, target) in enumerate(
@@ -154,6 +160,7 @@
     ]
     for load in loads + tile_loads:
         load.start()
+    part[ITERS] = jnp.zeros(part.shape[1:], f32)
     tiles[block_rows * slots] = jnp.zeros((tile, tile), bf16)
     half = block_rows // 2
     lanes = 128
@@ -192,9 +199,9 @@
         for copy in halo_copies(k, start):
             copy.start()
 
-    def copy1(k, turn, side):
+    def copy1(k, turn, side, source=None):
         return pltpu.make_async_remote_copy(
-            src_ref=part.at[k, 2 * turn + side],
+            src_ref=part.at[k, 2 * turn + side] if source is None else source,
             dst_ref=land1.at[k, 2 * turn + parity],
             send_sem=send1,
             recv_sem=recv1.at[k],
@@ -273,6 +280,7 @@
         return fold(total)
 
     spots = list(range(3 * block_rows))
+    last_chain = chains - 1
     own = spots[block_rows : 2 * block_rows]
     groups = ((0, range(half)), (half, range(half, block_rows)))
 
@@ -325,13 +333,50 @@
                 total = term if total is None else total + term
             total = fold(total) * scaling
             for side in range(2):
-                part[k, 2 * turn + side] = total[:, side * share : (side + 1) * share]
+                piece = total[:, side * share : (side + 1) * share]
+                if k < ITERS:
+                    part[k, 2 * turn + side] = piece
+                else:
+                    direct[2 * turn + side] = piece
+        if k < ITERS:
+            for turn, side in sides:
+                copy1(k, turn, side).start()
+        else:
+            pl.when(trailing)(send_straight)
+            pl.when(jnp.logical_not(trailing))(send_team)
+
+    def copy4(chain_number, turn, side):
+        number = 2 * pair_to[turn] + side
+        end = jnp.where(me == 0, 0, 1)
+        return pltpu.make_async_remote_copy(
+            src_ref=direct.at[2 * turn + side],
+            dst_ref=straight.at[end],
+            send_sem=send4,
+            recv_sem=recv4.at[end],
+            device_id=(chain_number * mates + lax.div(number, cols), lax.rem(number, cols)),
+            device_id_type=MESH,
+        )
+
+    def send_zeros():
         for turn, side in sides:
-            copy1(k, turn, side).start()
+            copy1(ITERS, turn, side).start()
+
+    def send_team():
+        for turn, side in sides:
+            copy1(ITERS, turn, side, direct.at[2 * turn + side]).start()
+
+    def send_straight():
+        for far in range(chains - 1):
+            for turn in range(team // 2):
+                for side in range(2):
+                    copy4(jnp.where(me == 0, last_chain - far, far), turn, side).start()
+        for turn, side in sides:
+            copy4(chain, turn, side).start()
+        straight[jnp.where(me == 0, 0, 1)] = direct[parity]
 
     def stage2(k):
         whole(land1.at[k, pl.ds(0, team - 1)], send1, recv1.at[k]).wait_recv()
-        total = part[k, parity]
+        total = part[k, parity] if k < ITERS else jnp.where(trailing, 0.0, direct[parity])
         for turn, side in sides:
             total = total + land1[k, 2 * turn + side]
         land2[k, chain] = total
@@ -343,6 +388,11 @@
         total = land2[k, 0]
         for r in range(1, chains):
             total = total + land2[k, r]
+        if k == ITERS:
+            for end in range(2):
+                await_end = whole(straight.at[end], send4, recv4.at[end]).wait_recv
+                pl.when(me != end * last)(await_end)
+            total = total + straight[0] + straight[1]
         return total
 
     for k in range(ITERS):
@@ -353,14 +403,20 @@
             stage1(m, [window[m, block_rows + b] for b in range(block_rows)])
         for m in range(0 if k == 2 else max(k - 1, 1), k):
             stage2(m)
+        if k == ITERS - 1:
+
+            @pl.when(trailing)
+            def _():
+                send_zeros()
+                stage2(ITERS - 1)
+
         pl.when(me < devices // 2)(functools.partial(left_last, k))
         pl.when(me >= devices // 2)(functools.partial(right_last, k))
+    sketches = [gathered(0)]
     stage1(ITERS, [window[ITERS, block_rows + b] for b in range(block_rows)])
-    stage2(ITERS - 1)
+    pl.when(jnp.logical_not(trailing))(functools.partial(stage2, ITERS - 1))
 
     lane = lax.broadcasted_iota(jnp.int32, (systems, lanes), 1)
-    sketches = []
-
     def pair_sums(pairs):
         packed = jnp.zeros((systems, lanes), f32)
         for p, (i, j) in enumerate(pairs):
@@ -383,7 +439,7 @@
 
     early = [(i, j) for i in range(ITERS) for j in range(i + 1)]
     late = [(ITERS, j) for j in range(ITERS + 1)]
-    for k in range(ITERS - 1):
+    for k in range(1, ITERS - 1):
         sketches.append(gathered(k))
     stage2(ITERS)
     sketches.append(gathered(ITERS - 1))
@@ -486,6 +542,7 @@
     whole(part.at[:, pl.ds(0, team - 1)], send1, recv1.at[0]).wait_send()
     whole(land2.at[:, pl.ds(0, chains - 1)], send2, recv2.at[0]).wait_send()
     whole(grams.at[:, pl.ds(0, team - 1)], send3, recv3.at[0]).wait_send()
+    pl.when(trailing)(whole(direct.at[pl.ds(0, last)], send4, recv4.at[0]).wait_send)
 
 
 def deliver(*refs):
@@ -539,6 +596,8 @@
             pltpu.VMEM((vectors, team, systems, share), f32),
             pltpu.VMEM((vectors, team, systems, share), f32),
             pltpu.VMEM((vectors, chains, systems, share), f32),
+            pltpu.VMEM((rows * cols, systems, share), f32),
+            pltpu.VMEM((2, systems, share), f32),
             pltpu.VMEM((2, team, systems, 128), f32),
             dma((6,)),
             dma,
@@ -548,6 +607,8 @@
             dma((vectors,)),
             dma,
             dma((vectors,)),
+            dma,
+            dma((2,)),
             dma,
             dma((2,)),
         ],

time: 35 us -> 34.6 us (0.989)
  Pallas kernels: 34.2 us -> 33.7 us
    pallas_call x1, Pallas kernels: 33.5 us -> 33.1 us  [local(): pl.pallas_call(functools.partial(kernel, rows, cols, scaling), out_shape=...]
where the time goes in v5:
time: 34.6 us; the launch traced here: 34.4 us
  Pallas kernels  33.7 us (97%)
  between operations  0.64 us (2%)
    pallas_call x1, Pallas kernels, local(): pl.pallas_call(functools.partial(kernel, rows, cols, scaling), out_shape=...  33.1 us

profile of v5, /device:TPU:0, one launch (start us, length us, event | category | flops | bytes accessed | tf_op | source)
XLA Modules:
  0.0 34.4 jit_solution(7684326792433862095)
XLA Ops:
  0.6 33.1 %shard_map.94 = (f32[16,1024]{1,0:T(8,128)S(1)}, f32[16,1024]{1,0:T(8,128)S(1)}, f32[5,4,16]{2,1,0:T(4,128)S(1)}) custom-call(s32[4,8]{1,0:T(4,128)} %columns_hbm.1, s32[4]{0:T(128)} %counts_hbm.1, f32[1,1024]{1,0:T(1,128)} %bitcast.4, s32[1,1024]{1,0:T(1,128)} %bitcast.5, s32[1,1024]{1,0:T(1,128)} %bitcast.6, f32[16,1024]{1,0:T(8,128)} %right_hbm.1, ...), custom_call_target="tpu_custom_call" | custom-call | tf_op jit(solution)/shard_map/pallas_call | solution.py:575
  33.7 0.7 %shard_map.95 = (f32[16,1024]{1,0:T(8,128)}, f32[16,1024]{1,0:T(8,128)}, f32[5,4,16]{2,1,0:T(4,128)}) custom-call(f32[16,1024]{1,0:T(8,128)S(1)} %get-tuple-element.9.refs_0_, f32[16,1024]{1,0:T(8,128)S(1)} %get-tuple-element.10.refs_1_, f32[5,4,16]{2,1,0:T(4,128)S(1)} %get-tuple-element.11.refs_2_), custom_call_target="tpu_custom_call" | custom-call | tf_op jit(solution)/shard_map/pallas_call | solution.py:627

commit v6 on v5

--- a/solution.py
+++ b/solution.py
@@ -280,7 +280,6 @@
         return fold(total)
 
     spots = list(range(3 * block_rows))
-    last_chain = chains - 1
     own = spots[block_rows : 2 * block_rows]
     groups = ((0, range(half)), (half, range(half, block_rows)))
 
@@ -342,7 +341,8 @@
             for turn, side in sides:
                 copy1(k, turn, side).start()
         else:
-            pl.when(trailing)(send_straight)
+            pl.when(me == 0)(functools.partial(send_straight, range(1, chains), True))
+            pl.when(me == last)(functools.partial(send_straight, range(chains - 1), False))
             pl.when(jnp.logical_not(trailing))(send_team)
 
     def copy4(chain_number, turn, side):
@@ -365,14 +365,12 @@
         for turn, side in sides:
             copy1(ITERS, turn, side, direct.at[2 * turn + side]).start()
 
-    def send_straight():
-        for far in range(chains - 1):
-            for turn in range(team // 2):
-                for side in range(2):
-                    copy4(jnp.where(me == 0, last_chain - far, far), turn, side).start()
-        for turn, side in sides:
-            copy4(chain, turn, side).start()
-        straight[jnp.where(me == 0, 0, 1)] = direct[parity]
+    def send_straight(others, own_first):
+        order = [(number, (turn, side)) for number in others for turn in range(team // 2) for side in range(2)]
+        mine = [(chain, seat_of) for seat_of in sides]
+        for number, (turn, side) in mine + order if own_first else order + mine:
+            copy4(number, turn, side).start()
+        straight[0 if own_first else 1] = direct[parity]
 
     def stage2(k):
         whole(land1.at[k, pl.ds(0, team - 1)], send1, recv1.at[k]).wait_recv()
@@ -405,6 +403,8 @@
             stage2(m)
         if k == ITERS - 1:
 
+            sketches = [gathered(0)]
+
             @pl.when(trailing)
             def _():
                 send_zeros()
@@ -412,7 +412,6 @@
 
         pl.when(me < devices // 2)(functools.partial(left_last, k))
         pl.when(me >= devices // 2)(functools.partial(right_last, k))
-    sketches = [gathered(0)]
     stage1(ITERS, [window[ITERS, block_rows + b] for b in range(block_rows)])
     pl.when(jnp.logical_not(trailing))(functools.partial(stage2, ITERS - 1))
 

time: 34.6 us -> 34.5 us (level)
  no operation moved by 1% of the time
where the time goes in v6:
time: 34.5 us; the launch traced here: 34.4 us
  Pallas kernels  33.7 us (98%)
  between operations  0.64 us (2%)
    pallas_call x1, Pallas kernels, local(): pl.pallas_call(functools.partial(kernel, rows, cols, scaling), out_shape=...  33.1 us

profile of v6, /device:TPU:0, one launch (start us, length us, event | category | flops | bytes accessed | tf_op | source)
XLA Modules:
  0.0 34.4 jit_solution(8421851030756551121)
XLA Ops:
  0.6 33.1 %shard_map.94 = (f32[16,1024]{1,0:T(8,128)S(1)}, f32[16,1024]{1,0:T(8,128)S(1)}, f32[5,4,16]{2,1,0:T(4,128)S(1)}) custom-call(s32[4,8]{1,0:T(4,128)} %columns_hbm.1, s32[4]{0:T(128)} %counts_hbm.1, f32[1,1024]{1,0:T(1,128)} %bitcast.4, s32[1,1024]{1,0:T(1,128)} %bitcast.5, s32[1,1024]{1,0:T(1,128)} %bitcast.6, f32[16,1024]{1,0:T(8,128)} %right_hbm.1, ...), custom_call_target="tpu_custom_call" | custom-call | tf_op jit(solution)/shard_map/pallas_call | solution.py:574
  33.7 0.7 %shard_map.95 = (f32[16,1024]{1,0:T(8,128)}, f32[16,1024]{1,0:T(8,128)}, f32[5,4,16]{2,1,0:T(4,128)}) custom-call(f32[16,1024]{1,0:T(8,128)S(1)} %get-tuple-element.9.refs_0_, f32[16,1024]{1,0:T(8,128)S(1)} %get-tuple-element.10.refs_1_, f32[5,4,16]{2,1,0:T(4,128)S(1)} %get-tuple-element.11.refs_2_), custom_call_target="tpu_custom_call" | custom-call | tf_op jit(solution)/shard_map/pallas_call | solution.py:626
